TPU v7x, 16 devices: a 4x2x1 block of a 4x4x8 slice. The times are simulated.
16 devices in a mesh: dp: 2 (over y, z), tp: 8 (over x, core).
Axes of the slice: x: 4, y: 2, z: 1, core: 2. Of those that a mesh axis runs over, the one named last changes fastest.
The devices are a block of a 4x4x8 slice.
Arguments:
- queries: bfloat16 [256, 256], P(('dp', 'tp')), parts along dimension 0
- w_first: bfloat16 [256, 1024], replicated
- w_second: bfloat16 [1024, 256], replicated
- catalogue: bfloat16 [262144, 256], P('tp')
- log_q: float32 [262144], P('tp')
- labels: int32 [256], P(('dp', 'tp')), parts along dimension 0
Outputs:
- output 1: float32 [2], P('dp'), parts along dimension 0
- output 2: bfloat16 [524288, 256], P(('dp', 'tp')), parts along dimension 0
- output 3: bfloat16 [512, 1024], P('dp'), parts along dimension 0
- output 4: bfloat16 [2048, 256], P('dp'), parts along dimension 0
There are 2 independent parts. A program takes and returns all parts, laid end to end along the dimension named above; an argument that names none is the same for every part.
All inputs are finite; a program needn't handle non-finite values.
Results may differ from a plain program's by a relative error of at most 0.00349722.
Values are sent between devices in bfloat16 or wider.
A program may use at most 768 MiB of HBM per device.

v0:
```python
import functools

import jax
import jax.numpy as jnp
from jax import lax
from jax.experimental import pallas as pl
from jax.experimental.pallas import tpu as pltpu
from jax.sharding import PartitionSpec as P

F32, BF16 = jnp.float32, jnp.bfloat16
MESH = pl.DeviceIdType.MESH
LANES = 128
TILE = 2048
UNROLL = 4
DOT_TILE = 512
GROUP = 32
WEIGHT_TILE = 4096
WEIGHT_GROUP = 16
SECOND_TILE = 8192
LOAD_TILE = 4096
OUT_TILE = 4096
EARLY = 5
SHIFT = 16
LOWEST = -3.0e38


def dot(a, b, contract):
    return lax.dot_general(a, b, ((contract[:1], contract[1:]), ((), ())), preferred_element_type=F32)


def loss_kernel(n, q_hbm, w1_hbm, w2_hbm, cat_hbm, lq_hbm, lab_hbm,
                cat, dx_ref, h_ref, a_ref, q_ref, w2_ref, loss_ref,
                x_ref, g_ref, ez, z_even, z_odd, lq, w1, labels, lab, d, m_run, s_run, t_run, m_hist, stats, targets, part, pieces,
                load_sem, cat_sem, send_sem, recv_sem):
    me = lax.axis_index("tp")
    own = q_hbm.shape[0]
    rows = own * n
    items = cat_hbm.shape[0]
    tiles = items // TILE
    chunks = TILE // LANES
    my_rows = pl.ds(pl.multiple_of(me * own, own), own)

    others = pl.ds(0, n - 1)
    other_rows = pl.ds(0, rows - own)

    q_load = pltpu.make_async_copy(q_hbm, q_ref.at[my_rows], load_sem.at[0])
    w1_load = pltpu.make_async_copy(w1_hbm, w1, load_sem.at[1])
    w2_load = pltpu.make_async_copy(w2_hbm, w2_ref, load_sem.at[2])
    lq_load = pltpu.make_async_copy(lq_hbm, lq, load_sem.at[3])
    lab_load = pltpu.make_async_copy(lab_hbm, labels, load_sem.at[4])
    for load in (q_load, w1_load, w2_load):
        load.start()
    barrier = pltpu.get_barrier_semaphore()
    peers = [lax.rem(me + k, n) for k in range(1, n)]
    for p in peers:
        pl.semaphore_signal(barrier, inc=1, device_id={"tp": p}, device_id_type=MESH)
    for load in (lq_load, lab_load):
        load.start()

    def cat_copy(k):
        part_rows = pl.ds(pl.multiple_of(k * LOAD_TILE, LOAD_TILE), LOAD_TILE)
        return pltpu.make_async_copy(cat_hbm.at[part_rows], cat.at[part_rows], cat_sem.at[k])

    q_load.wait()
    w1_load.wait()
    w2_load.wait()
    for k in range(items // LOAD_TILE):
        cat_copy(k).start()
    own_hidden = jnp.maximum(dot(q_ref[my_rows, :], w1[...], (1, 0)), 0.0).astype(BF16)
    x_ref[my_rows, :] = dot(own_hidden, w2_ref[...], (1, 0)).astype(BF16)
    pl.semaphore_wait(barrier, n - 1)

    def exchange(src, dst, stage):
        for p in peers:
            pltpu.make_async_remote_copy(
                src_ref=src(p), dst_ref=dst, send_sem=send_sem.at[stage], recv_sem=recv_sem.at[stage],
                device_id={"tp": p}, device_id_type=MESH).start()

    def arrive(others, stage):
        pltpu.make_async_copy(others, others, recv_sem.at[stage]).wait()

    def sent(others, stage):
        pltpu.make_async_copy(others, others, send_sem.at[stage]).wait()

    def rows_of(p):
        return pl.ds(pl.multiple_of(p * own, own), own)

    exchange(lambda p: x_ref.at[my_rows], x_ref.at[my_rows], 1)
    lq_load.wait()
    lab_load.wait()
    for r in range(own):
        lab[pl.ds(me * own + r, 1), :] = jnp.full((1, LANES), labels[r], jnp.int32)
    m_run[...] = jnp.full(m_run.shape, LOWEST, F32)
    s_run[...] = jnp.zeros(s_run.shape, F32)
    part[...] = jnp.zeros(part.shape, F32)
    arrive(x_ref.at[other_rows], 1)

    def logits(i, z_ref):
        for j in range(TILE // DOT_TILE):
            base = pl.multiple_of(i * TILE + j * DOT_TILE, DOT_TILE)
            z = dot(x_ref[...], cat[pl.ds(base, DOT_TILE), :], (1, 1)) - lq[:, pl.ds(base, DOT_TILE)]
            m = m_run[...]
            for c in range(DOT_TILE // LANES):
                zc = z[:, c * LANES:(c + 1) * LANES]
                z_ref[pl.ds(SHIFT + (j * (DOT_TILE // LANES) + c) * rows, rows), :] = zc
                ez[i * chunks + j * (DOT_TILE // LANES) + c] = zc
                m = jnp.maximum(m, zc)
            m_run[...] = m
            yield
        m_hist[i + 1] = m

    def weigh(i, z_ref):
        for r in range(0, rows, GROUP):
            at = slice(r, r + GROUP)
            m = m_hist[i + 1, at, :]
            s = s_run[at, :] * jnp.exp(m_hist[i, at, :] - m)
            for c in range(chunks):
                s = s + jnp.exp(z_ref[pl.ds(SHIFT + c * rows + r, GROUP), :] - m)
            s_run[at, :] = s
            yield

    def arrived(j):
        for k in range(UNROLL * TILE // LOAD_TILE):
            cat_copy(j * (UNROLL * TILE // LOAD_TILE) + k).wait()

    def together(*parts):
        parts = list(parts)
        while parts:
            parts = [p for p in parts if next(p, parts) is not parts]

    z_refs = (z_even, z_odd)

    def step(i, k):
        together(logits(i + 1, z_refs[(k + 1) % 2]), weigh(i, z_refs[k % 2]))

    m_hist[0] = m_run[...]
    arrived(0)
    together(logits(0, z_even))
    exchange(lambda p: lab.at[my_rows], lab.at[my_rows], 0)
    exchange(lambda p: q_ref.at[my_rows], q_ref.at[my_rows], 6)

    def first_pass(j, carry):
        arrived(j + 1)
        for k in range(UNROLL):
            step(j * UNROLL + k, k)
        return carry

    lax.fori_loop(0, tiles // UNROLL - 1, first_pass, 0)
    for k in range(UNROLL - 1):
        step(tiles - UNROLL + k, k)
    together(weigh(tiles - 1, z_odd))

    m_t = m_run[...].T
    m_row = jnp.max(m_t, axis=0, keepdims=True)
    s_row = jnp.sum(s_run[...].T * jnp.exp(m_t - m_row), axis=0, keepdims=True)
    sub = lax.broadcasted_iota(jnp.int32, (8, LANES), 0)
    stats[me] = jnp.where(sub == 0, m_row, s_row)
    exchange(lambda p: stats.at[me], stats.at[me], 2)
    t_run[...] = jnp.zeros(t_run.shape, F32)
    arrive(lab.at[other_rows], 0)
    local = lab[...] - me * items
    lane = lax.broadcasted_iota(jnp.int32, lab.shape, 1)
    d[...] = local - lane
    wide = WEIGHT_TILE // LANES

    def weights(i, carry):
        for r in range(0, rows, WEIGHT_GROUP):
            at = slice(r, r + WEIGHT_GROUP)
            m = m_run[at, :]
            t = t_run[at, :]
            dd = d[at, :] - i * WEIGHT_TILE
            for c in range(wide):
                zc = ez[i * wide + c, at, :]
                t = jnp.where(dd == c * LANES, zc, t)
                ez[i * wide + c, at, :] = jnp.exp(zc - m)
            t_run[at, :] = t
        return carry

    lax.fori_loop(0, items // WEIGHT_TILE, weights, 0)
    t_col = jnp.broadcast_to(jnp.sum(t_run[...], axis=1, keepdims=True), lab.shape)
    targets[me] = t_col.T[0:8, :]
    arrive(stats.at[others], 2)
    big = stats[0, 0:1, :]
    for p in range(1, n):
        big = jnp.maximum(big, stats[p, 0:1, :])
    total = jnp.zeros_like(big)
    for p in range(n):
        total = total + stats[p, 1:2, :] * jnp.exp(stats[p, 0:1, :] - big)
    inv = 1.0 / (total * rows)
    big_col = jnp.broadcast_to(big, (rows, LANES)).T
    inv_col = jnp.broadcast_to(inv, (rows, LANES)).T
    hit_col = (jnp.exp(t_col - big_col) * inv_col - 1.0 / rows).astype(BF16)
    scale = jnp.exp(m_run[...] - big_col) * inv_col
    home = jnp.where(local - local // LANES * LANES == lane, local // LANES, -1)
    home = jnp.where((local >= 0) & (local < items), home, -1).astype(F32)

    def second_pass(i, carry):
        gs = []
        count = SECOND_TILE // LANES
        here = (home - (i * count).astype(F32)).astype(BF16)
        for c in range(count):
            g = (ez[i * count + c] * scale).astype(BF16)
            g = jnp.where(here == jnp.bfloat16(c), hit_col, g)
            g_ref[i * count + c, :rows, :] = g
            gs.append(g)
        base = pl.multiple_of(i * SECOND_TILE, SECOND_TILE)
        part[...] += dot(jnp.concatenate(gs, axis=1), cat[pl.ds(base, SECOND_TILE), :], (1, 0))
        return carry

    lax.fori_loop(0, items // SECOND_TILE, second_pass, 0)

    exchange(lambda p: part.at[rows_of(p)], pieces.at[me], 3)
    pieces[me] = part[my_rows, :]

    def item_grads(i, carry):
        count = OUT_TILE // LANES
        g = jnp.concatenate([g_ref[i * count + c, :rows, :] for c in range(count)], axis=1)
        cat[pl.ds(pl.multiple_of(i * OUT_TILE, OUT_TILE), OUT_TILE), :] = dot(g, x_ref[...], (0, 0)).astype(BF16)
        return carry

    lax.fori_loop(0, EARLY, item_grads, 0)
    exchange(lambda p: targets.at[me], targets.at[me], 5)
    arrive(pieces.at[others], 3)
    acc = pieces[0]
    for p in range(1, n):
        acc = acc + pieces[p]
    dx_ref[my_rows, :] = acc.astype(BF16)
    exchange(lambda p: dx_ref.at[my_rows], dx_ref.at[my_rows], 4)
    lax.fori_loop(EARLY, items // OUT_TILE, item_grads, 0)
    arrive(q_ref.at[other_rows], 6)
    a = dot(q_ref[...], w1[...], (1, 0))
    a_ref[...] = a
    h_ref[...] = jnp.maximum(a, 0.0).astype(BF16)
    arrive(dx_ref.at[other_rows], 4)
    arrive(targets.at[others], 5)
    target = targets[0, 0:1, :]
    for p in range(1, n):
        target = target + targets[p, 0:1, :]
    loss_ref[...] = jnp.broadcast_to(
        jnp.sum(big + jnp.log(total) - target, axis=1, keepdims=True) / rows, loss_ref.shape)
    sent(lab.at[other_rows], 0)
    sent(x_ref.at[other_rows], 1)
    sent(q_ref.at[other_rows], 6)
    sent(stats.at[others], 2)
    sent(pieces.at[others], 3)
    sent(dx_ref.at[other_rows], 4)
    sent(targets.at[others], 5)


def grad_kernel(de_ref, dx_ref, h_ref, a_ref, q_ref, w2_ref, loss_ref,
                loss_hbm, de_hbm, dw1_hbm, dw2_hbm, loss, dw1, dw2, sem):
    copies = []
    for k in range(de_hbm.shape[0] // LOAD_TILE):
        at = pl.ds(k * LOAD_TILE, LOAD_TILE)
        pltpu.make_async_copy(de_ref.at[at], de_hbm.at[at], sem.at[3]).start()
    dx = dx_ref[...]
    dw2[...] = dot(h_ref[...], dx, (0, 0)).astype(BF16)
    dh = dot(dx, w2_ref[...], (1, 1))
    da = jnp.where(a_ref[...] > 0.0, dh, 0.0).astype(BF16)
    dw1[...] = dot(q_ref[...], da, (0, 0)).astype(BF16)
    loss[...] = loss_ref[0:1, 0:1]
    copies.append(pltpu.make_async_copy(loss, loss_hbm, sem.at[0]))
    copies.append(pltpu.make_async_copy(dw1, dw1_hbm, sem.at[1]))
    copies.append(pltpu.make_async_copy(dw2, dw2_hbm, sem.at[2]))
    for copy in copies[-3:]:
        copy.start()
    for copy in copies:
        copy.wait()
    pltpu.make_async_copy(de_ref, de_hbm, sem.at[3]).wait()


def solution(mesh):
    n = mesh.shape["tp"]

    def local_step(queries, w_first, w_second, catalogue, log_q, labels):
        own, d_in = queries.shape
        hid, emb = w_second.shape
        items = catalogue.shape[0]
        rows = own * n
        hbm = pl.BlockSpec(memory_space=pl.ANY)
        vmem = pl.BlockSpec(memory_space=pltpu.VMEM)
        dma = pltpu.SemaphoreType.DMA
        held = pl.pallas_call(
            functools.partial(loss_kernel, n),
            name="loss_kernel",
            out_shape=[
                pltpu.VMEM((items, emb), BF16),
                pltpu.VMEM((rows, emb), BF16),
                pltpu.VMEM((rows, hid), BF16),
                pltpu.VMEM((rows, hid), F32),
                pltpu.VMEM((rows, d_in), BF16),
                pltpu.VMEM((hid, emb), BF16),
                pltpu.VMEM((32, LANES), F32),
            ],
            in_specs=[hbm] * 6,
            out_specs=[vmem] * 7,
            scratch_shapes=[
                pltpu.VMEM((rows, emb), BF16),
                pltpu.VMEM((items // LANES, rows + SHIFT, LANES), BF16),
                pltpu.VMEM((items // LANES, rows, LANES), F32),
                pltpu.VMEM((2 * SHIFT + TILE // LANES * rows, LANES), F32),
                pltpu.VMEM((2 * SHIFT + TILE // LANES * rows, LANES), F32),
                pltpu.VMEM((1, items), F32),
                pltpu.VMEM((d_in, hid), BF16),
                pltpu.SMEM((own,), jnp.int32),
                pltpu.VMEM((rows, LANES), jnp.int32),
                pltpu.VMEM((rows, LANES), jnp.int32),
                pltpu.VMEM((rows, LANES), F32),
                pltpu.VMEM((rows, LANES), F32),
                pltpu.VMEM((rows, LANES), F32),
                pltpu.VMEM((items // TILE + 1, rows, LANES), F32),
                pltpu.VMEM((n, 8, LANES), F32),
                pltpu.VMEM((n, 8, LANES), F32),
                pltpu.VMEM((rows, emb), F32),
                pltpu.VMEM((n, own, emb), F32),
                dma((5,)),
                dma((items // LOAD_TILE,)),
                dma((7,)),
                dma((7,)),
            ],
            compiler_params=pltpu.CompilerParams(collective_id=0, has_side_effects=True, vmem_limit_bytes=44 << 20),
        )(queries, w_first, w_second, catalogue, log_q.reshape(1, items), labels)
        loss, grad_items, grad_first, grad_second = pl.pallas_call(
            grad_kernel,
            name="grad_kernel",
            out_shape=[
                jax.ShapeDtypeStruct((1, 1), F32),
                jax.ShapeDtypeStruct((items, emb), BF16),
                jax.ShapeDtypeStruct((d_in, hid), BF16),
                jax.ShapeDtypeStruct((hid, emb), BF16),
            ],
            in_specs=[vmem] * 7,
            out_specs=[hbm] * 4,
            scratch_shapes=[
                pltpu.VMEM((1, 1), F32),
                pltpu.VMEM((d_in, hid), BF16),
                pltpu.VMEM((hid, emb), BF16),
                dma((4,)),
            ],
            compiler_params=pltpu.CompilerParams(vmem_limit_bytes=24 << 20),
        )(*held)
        return loss.reshape(1), grad_items, grad_first, grad_second

    row_spec = P(("dp", "tp"), None)
    return jax.shard_map(
        local_step, mesh=mesh,
        in_specs=(row_spec, P(None, None), P(None, None), P("tp", None), P("tp"), P(("dp", "tp"))),
        out_specs=(P("dp"), row_spec, P("dp", None), P("dp", None)), check_vma=False)
```

profile of v0, /device:TPU:113, one launch (start us, length us, event | category | flops | bytes accessed | tf_op | source)
XLA Modules:
  0.0 36.9 jit_solution(10884544747341894659)
XLA Ops:
  0.6 29.9 %loss_kernel.1 = (bf16[32768,256]{1,0:T(8,128)(2,1)S(1)}, bf16[128,256]{1,0:T(8,128)(2,1)S(1)}, bf16[128,1024]{1,0:T(8,128)(2,1)S(1)}, f32[128,1024]{1,0:T(8,128...) custom-call(bf16[16,256]{1,0:T(8,128)(2,1)} %q_hbm.1, ...), custom_call_target="tpu_custom_call" | custom-call | tf_op jit(solution)/shard_map/loss_kernel/pallas_call | solution.py:283
  30.5 6.4 %grad_kernel.1 = (f32[1,1]{1,0:T(1,128)}, bf16[32768,256]{1,0:T(8,128)(2,1)}, bf16[256,1024]{1,0:T(8,128)(2,1)}, bf16[1024,256]{1,0:T(8,128)(2,1)}) custom-call(bf16[32768,256]{1,0:T(8,128)(2,1)S(1)} %get-tuple-element.15.de_ref, bf16[128,256]{1,0:T(8,128)(2,1)S(1)} %get-tuple-element.16.dx_ref, bf16[128,1024]{1,0:T(8,128)(2,1)S(1)} %get-tuple-element.17.h_ref, ...), custom_call_target="tpu_custom_call" | custom-call | tf_op jit(solution)/shard_map/grad_kernel/pallas_call | solution.py:323
where the time goes:
time: 37 us; the launch traced here: 36.9 us
  Pallas kernels  36.3 us (98%)
  between operations  0.64 us (2%)
    pallas_call x1, Pallas kernels, local_step(): pl.pallas_call(functools.partial(loss_kernel, n), name='loss_kernel', out...  29.9 us
    pallas_call x1, Pallas kernels, local_step(): pl.pallas_call(grad_kernel, name='grad_kernel', out_shape=[jax.ShapeDtype...  6.38 us

commit v1 on v0

--- a/solution.py
+++ b/solution.py
@@ -51,7 +51,7 @@
     for load in (q_load, w1_load, w2_load):
         load.start()
     barrier = pltpu.get_barrier_semaphore()
-    peers = [lax.rem(me + k, n) for k in range(1, n)]
+    peers = [lax.rem(me + k, n) for k in sorted(range(1, n), key=lambda k: -min(k, n - k))]
     for p in peers:
         pl.semaphore_signal(barrier, inc=1, device_id={"tp": p}, device_id_type=MESH)
     for load in (lq_load, lab_load):
@@ -250,9 +250,13 @@
 def grad_kernel(de_ref, dx_ref, h_ref, a_ref, q_ref, w2_ref, loss_ref,
                 loss_hbm, de_hbm, dw1_hbm, dw2_hbm, loss, dw1, dw2, sem):
     copies = []
-    for k in range(de_hbm.shape[0] // LOAD_TILE):
-        at = pl.ds(k * LOAD_TILE, LOAD_TILE)
+
+    def start_copy(k, carry):
+        at = pl.ds(pl.multiple_of(k * LOAD_TILE, LOAD_TILE), LOAD_TILE)
         pltpu.make_async_copy(de_ref.at[at], de_hbm.at[at], sem.at[3]).start()
+        return carry
+
+    lax.fori_loop(0, de_hbm.shape[0] // LOAD_TILE, start_copy, 0)
     dx = dx_ref[...]
     dw2[...] = dot(h_ref[...], dx, (0, 0)).astype(BF16)
     dh = dot(dx, w2_ref[...], (1, 1))

time: 37 us -> 36.4 us (0.984)
  Pallas kernels: 36.3 us -> 35.6 us
    pallas_call x1, Pallas kernels: 29.9 us -> 29.5 us  [local_step(): pl.pallas_call(functools.partial(loss_kernel, n), name='loss_kernel', out...]
where the time goes in v1:
time: 36.4 us; the launch traced here: 36.3 us
  Pallas kernels  35.6 us (98%)
  between operations  0.64 us (2%)
    pallas_call x1, Pallas kernels, local_step(): pl.pallas_call(functools.partial(loss_kernel, n), name='loss_kernel', out...  29.5 us
    pallas_call x1, Pallas kernels, local_step(): pl.pallas_call(grad_kernel, name='grad_kernel', out_shape=[jax.ShapeDtype...  6.16 us

profile of v1, /device:TPU:113, one launch (start us, length us, event | category | flops | bytes accessed | tf_op | source)
XLA Modules:
  0.0 36.3 jit_solution(8339210768205209764)
XLA Ops:
  0.6 29.5 %loss_kernel.1 = (bf16[32768,256]{1,0:T(8,128)(2,1)S(1)}, bf16[128,256]{1,0:T(8,128)(2,1)S(1)}, bf16[128,1024]{1,0:T(8,128)(2,1)S(1)}, f32[128,1024]{1,0:T(8,128...) custom-call(bf16[16,256]{1,0:T(8,128)(2,1)} %q_hbm.1, ...), custom_call_target="tpu_custom_call" | custom-call | tf_op jit(solution)/shard_map/loss_kernel/pallas_call | solution.py:287
  30.1 6.2 %grad_kernel.1 = (f32[1,1]{1,0:T(1,128)}, bf16[32768,256]{1,0:T(8,128)(2,1)}, bf16[256,1024]{1,0:T(8,128)(2,1)}, bf16[1024,256]{1,0:T(8,128)(2,1)}) custom-call(bf16[32768,256]{1,0:T(8,128)(2,1)S(1)} %get-tuple-element.15.de_ref, bf16[128,256]{1,0:T(8,128)(2,1)S(1)} %get-tuple-element.16.dx_ref, bf16[128,1024]{1,0:T(8,128)(2,1)S(1)} %get-tuple-element.17.h_ref, ...), custom_call_target="tpu_custom_call" | custom-call | tf_op jit(solution)/shard_map/grad_kernel/pallas_call | solution.py:327

commit v2 on v1

--- a/solution.py
+++ b/solution.py
@@ -13,10 +13,10 @@
 TILE = 2048
 UNROLL = 4
 DOT_TILE = 512
-GROUP = 32
+GROUP = 16
 WEIGHT_TILE = 4096
 WEIGHT_GROUP = 16
-SECOND_TILE = 8192
+SECOND_TILE = 16384
 LOAD_TILE = 4096
 OUT_TILE = 4096
 EARLY = 5
@@ -30,7 +30,7 @@
 
 def loss_kernel(n, q_hbm, w1_hbm, w2_hbm, cat_hbm, lq_hbm, lab_hbm,
                 cat, dx_ref, h_ref, a_ref, q_ref, w2_ref, loss_ref,
-                x_ref, g_ref, ez, z_even, z_odd, lq, w1, labels, lab, d, m_run, s_run, t_run, m_hist, stats, targets, part, pieces,
+                x_ref, g_ref, ez, lq, w1, labels, lab, d, m_run, s_run, t_run, m_hist, stats, targets, part, pieces,
                 load_sem, cat_sem, send_sem, recv_sem):
     me = lax.axis_index("tp")
     own = q_hbm.shape[0]
@@ -95,27 +95,26 @@
     part[...] = jnp.zeros(part.shape, F32)
     arrive(x_ref.at[other_rows], 1)
 
-    def logits(i, z_ref):
-        for j in range(TILE // DOT_TILE):
-            base = pl.multiple_of(i * TILE + j * DOT_TILE, DOT_TILE)
-            z = dot(x_ref[...], cat[pl.ds(base, DOT_TILE), :], (1, 1)) - lq[:, pl.ds(base, DOT_TILE)]
+    def logits(j, k):
+        for p in range(TILE // DOT_TILE):
+            items_at = pl.ds(pl.multiple_of(j * UNROLL * TILE, TILE) + (k * TILE + p * DOT_TILE), DOT_TILE)
+            z = dot(x_ref[...], cat[items_at, :], (1, 1)) - lq[:, items_at]
             m = m_run[...]
             for c in range(DOT_TILE // LANES):
                 zc = z[:, c * LANES:(c + 1) * LANES]
-                z_ref[pl.ds(SHIFT + (j * (DOT_TILE // LANES) + c) * rows, rows), :] = zc
-                ez[i * chunks + j * (DOT_TILE // LANES) + c] = zc
+                ez[j * UNROLL * chunks + (k * chunks + p * (DOT_TILE // LANES) + c)] = zc
                 m = jnp.maximum(m, zc)
             m_run[...] = m
             yield
-        m_hist[i + 1] = m
-
-    def weigh(i, z_ref):
+        m_hist[j * UNROLL + (k + 1)] = m
+
+    def weigh(j, k):
         for r in range(0, rows, GROUP):
             at = slice(r, r + GROUP)
-            m = m_hist[i + 1, at, :]
-            s = s_run[at, :] * jnp.exp(m_hist[i, at, :] - m)
+            m = m_hist[j * UNROLL + (k + 1), at, :]
+            s = s_run[at, :] * jnp.exp(m_hist[j * UNROLL + k, at, :] - m)
             for c in range(chunks):
-                s = s + jnp.exp(z_ref[pl.ds(SHIFT + c * rows + r, GROUP), :] - m)
+                s = s + jnp.exp(ez[j * UNROLL * chunks + (k * chunks + c), at, :] - m)
             s_run[at, :] = s
             yield
 
@@ -128,27 +127,23 @@
         while parts:
             parts = [p for p in parts if next(p, parts) is not parts]
 
-    z_refs = (z_even, z_odd)
-
-    def step(i, k):
-        together(logits(i + 1, z_refs[(k + 1) % 2]), weigh(i, z_refs[k % 2]))
-
     m_hist[0] = m_run[...]
     arrived(0)
-    together(logits(0, z_even))
+    together(logits(0, 0))
     exchange(lambda p: lab.at[my_rows], lab.at[my_rows], 0)
     exchange(lambda p: q_ref.at[my_rows], q_ref.at[my_rows], 6)
 
     def first_pass(j, carry):
         arrived(j + 1)
         for k in range(UNROLL):
-            step(j * UNROLL + k, k)
-        return carry
-
-    lax.fori_loop(0, tiles // UNROLL - 1, first_pass, 0)
+            together(logits(j, k + 1), weigh(j, k))
+        return carry
+
+    trips = tiles // UNROLL - 1
+    lax.fori_loop(0, trips, first_pass, 0)
     for k in range(UNROLL - 1):
-        step(tiles - UNROLL + k, k)
-    together(weigh(tiles - 1, z_odd))
+        together(logits(trips, k + 1), weigh(trips, k))
+    together(weigh(trips, UNROLL - 1))
 
     m_t = m_run[...].T
     m_row = jnp.max(m_t, axis=0, keepdims=True)
@@ -302,8 +297,6 @@
                 pltpu.VMEM((rows, emb), BF16),
                 pltpu.VMEM((items // LANES, rows + SHIFT, LANES), BF16),
                 pltpu.VMEM((items // LANES, rows, LANES), F32),
-                pltpu.VMEM((2 * SHIFT + TILE // LANES * rows, LANES), F32),
-                pltpu.VMEM((2 * SHIFT + TILE // LANES * rows, LANES), F32),
                 pltpu.VMEM((1, items), F32),
                 pltpu.VMEM((d_in, hid), BF16),
                 pltpu.SMEM((own,), jnp.int32),

time: 36.4 us -> 36.4 us (level)
  no operation moved by 1% of the time
where the time goes in v2:
time: 36.4 us; the launch traced here: 36.2 us
  Pallas kernels  35.6 us (98%)
  between operations  0.64 us (2%)
    pallas_call x1, Pallas kernels, local_step(): pl.pallas_call(functools.partial(loss_kernel, n), name='loss_kernel', out...  29.4 us
    pallas_call x1, Pallas kernels, local_step(): pl.pallas_call(grad_kernel, name='grad_kernel', out_shape=[jax.ShapeDtype...  6.16 us

profile of v2, /device:TPU:113, one launch (start us, length us, event | category | flops | bytes accessed | tf_op | source)
XLA Modules:
  0.0 36.2 jit_solution(1212314812099635130)
XLA Ops:
  0.6 29.4 %loss_kernel.1 = (bf16[32768,256]{1,0:T(8,128)(2,1)S(1)}, bf16[128,256]{1,0:T(8,128)(2,1)S(1)}, bf16[128,1024]{1,0:T(8,128)(2,1)S(1)}, f32[128,1024]{1,0:T(8,128...) custom-call(bf16[16,256]{1,0:T(8,128)(2,1)} %q_hbm.1, ...), custom_call_target="tpu_custom_call" | custom-call | tf_op jit(solution)/shard_map/loss_kernel/pallas_call | solution.py:282
  30.1 6.2 %grad_kernel.1 = (f32[1,1]{1,0:T(1,128)}, bf16[32768,256]{1,0:T(8,128)(2,1)}, bf16[256,1024]{1,0:T(8,128)(2,1)}, bf16[1024,256]{1,0:T(8,128)(2,1)}) custom-call(bf16[32768,256]{1,0:T(8,128)(2,1)S(1)} %get-tuple-element.15.de_ref, bf16[128,256]{1,0:T(8,128)(2,1)S(1)} %get-tuple-element.16.dx_ref, bf16[128,1024]{1,0:T(8,128)(2,1)S(1)} %get-tuple-element.17.h_ref, ...), custom_call_target="tpu_custom_call" | custom-call | tf_op jit(solution)/shard_map/grad_kernel/pallas_call | solution.py:320

commit v3 on v1

--- a/solution.py
+++ b/solution.py
@@ -16,10 +16,10 @@
 GROUP = 32
 WEIGHT_TILE = 4096
 WEIGHT_GROUP = 16
-SECOND_TILE = 8192
+SECOND_TILE = 16384
 LOAD_TILE = 4096
 OUT_TILE = 4096
-EARLY = 5
+EARLY = 4
 SHIFT = 16
 LOWEST = -3.0e38
 

time: 36.4 us -> 35.7 us (0.981)
  Pallas kernels: 35.6 us -> 34.9 us
    pallas_call x1, Pallas kernels: 29.5 us -> 28.7 us  [local_step(): pl.pallas_call(functools.partial(loss_kernel, n), name='loss_kernel', out...]
where the time goes in v3:
time: 35.7 us; the launch traced here: 35.5 us
  Pallas kernels  34.9 us (98%)
  between operations  0.64 us (2%)
    pallas_call x1, Pallas kernels, local_step(): pl.pallas_call(functools.partial(loss_kernel, n), name='loss_kernel', out...  28.7 us
    pallas_call x1, Pallas kernels, local_step(): pl.pallas_call(grad_kernel, name='grad_kernel', out_shape=[jax.ShapeDtype...  6.16 us

profile of v3, /device:TPU:113, one launch (start us, length us, event | category | flops | bytes accessed | tf_op | source)
XLA Modules:
  0.0 35.5 jit_solution(5753327954829285373)
XLA Ops:
  0.6 28.7 %loss_kernel.1 = (bf16[32768,256]{1,0:T(8,128)(2,1)S(1)}, bf16[128,256]{1,0:T(8,128)(2,1)S(1)}, bf16[128,1024]{1,0:T(8,128)(2,1)S(1)}, f32[128,1024]{1,0:T(8,128...) custom-call(bf16[16,256]{1,0:T(8,128)(2,1)} %q_hbm.1, ...), custom_call_target="tpu_custom_call" | custom-call | tf_op jit(solution)/shard_map/loss_kernel/pallas_call | solution.py:287
  29.4 6.2 %grad_kernel.1 = (f32[1,1]{1,0:T(1,128)}, bf16[32768,256]{1,0:T(8,128)(2,1)}, bf16[256,1024]{1,0:T(8,128)(2,1)}, bf16[1024,256]{1,0:T(8,128)(2,1)}) custom-call(bf16[32768,256]{1,0:T(8,128)(2,1)S(1)} %get-tuple-element.15.de_ref, bf16[128,256]{1,0:T(8,128)(2,1)S(1)} %get-tuple-element.16.dx_ref, bf16[128,1024]{1,0:T(8,128)(2,1)S(1)} %get-tuple-element.17.h_ref, ...), custom_call_target="tpu_custom_call" | custom-call | tf_op jit(solution)/shard_map/grad_kernel/pallas_call | solution.py:327

commit v4 on v3

--- a/solution.py
+++ b/solution.py
@@ -18,8 +18,8 @@
 WEIGHT_GROUP = 16
 SECOND_TILE = 16384
 LOAD_TILE = 4096
-OUT_TILE = 4096
-EARLY = 4
+OUT_TILE = 8192
+EARLY = 2
 SHIFT = 16
 LOWEST = -3.0e38
 

time: 35.7 us -> 35.6 us (level)
  no operation moved by 1% of the time
where the time goes in v4:
time: 35.6 us; the launch traced here: 35.4 us
  Pallas kernels  34.8 us (98%)
  between operations  0.64 us (2%)
    pallas_call x1, Pallas kernels, local_step(): pl.pallas_call(functools.partial(loss_kernel, n), name='loss_kernel', out...  28.6 us
    pallas_call x1, Pallas kernels, local_step(): pl.pallas_call(grad_kernel, name='grad_kernel', out_shape=[jax.ShapeDtype...  6.16 us

profile of v4, /device:TPU:113, one launch (start us, length us, event | category | flops | bytes accessed | tf_op | source)
XLA Modules:
  0.0 35.4 jit_solution(13779574236451183969)
XLA Ops:
  0.6 28.6 %loss_kernel.1 = (bf16[32768,256]{1,0:T(8,128)(2,1)S(1)}, bf16[128,256]{1,0:T(8,128)(2,1)S(1)}, bf16[128,1024]{1,0:T(8,128)(2,1)S(1)}, f32[128,1024]{1,0:T(8,128...) custom-call(bf16[16,256]{1,0:T(8,128)(2,1)} %q_hbm.1, ...), custom_call_target="tpu_custom_call" | custom-call | tf_op jit(solution)/shard_map/loss_kernel/pallas_call | solution.py:287
  29.2 6.2 %grad_kernel.1 = (f32[1,1]{1,0:T(1,128)}, bf16[32768,256]{1,0:T(8,128)(2,1)}, bf16[256,1024]{1,0:T(8,128)(2,1)}, bf16[1024,256]{1,0:T(8,128)(2,1)}) custom-call(bf16[32768,256]{1,0:T(8,128)(2,1)S(1)} %get-tuple-element.15.de_ref, bf16[128,256]{1,0:T(8,128)(2,1)S(1)} %get-tuple-element.16.dx_ref, bf16[128,1024]{1,0:T(8,128)(2,1)S(1)} %get-tuple-element.17.h_ref, ...), custom_call_target="tpu_custom_call" | custom-call | tf_op jit(solution)/shard_map/grad_kernel/pallas_call | solution.py:327
